TPU v7x, 32 devices: a whole 2x2x4 slice. The times are simulated.
32 devices in a mesh: slab: 4 (over x, core), img: 8 (over z, y).
Axes of the slice: x: 2, y: 2, z: 4, core: 2. Of those that a mesh axis runs over, the one named last changes fastest.
Arguments:
- feats: bfloat16 [8, 32, 128, 512], P('img', 'slab'), may hold values from -6 to 6
- labels: int32 [8], P('img'), may hold values from 0 to 999
- conv_w: bfloat16 [9, 512, 4], replicated, may hold values from -0.09375 to 0.09375
- embed_w: bfloat16 [16, 1024], replicated, may hold values from -1.5 to 1.5
- mod_table: bfloat16 [1000, 2048], replicated, may hold values from -3 to 3
- qkv_w: bfloat16 [1024, 3072], replicated, may hold values from -0.1875 to 0.1875
- out_w: bfloat16 [1024, 1024], replicated, may hold values from -0.1875 to 0.1875
- proj_w: bfloat16 [1024, 768], replicated, may hold values from -0.1875 to 0.1875
- dino: bfloat16 [8, 1024, 768], P('img', 'slab'), may hold values from -6 to 6
Outputs:
- grad_feats: bfloat16 [8, 32, 128, 512], P('img', 'slab')
- grad_proj: float32 [1024, 768], replicated
- grad_conv: float32 [9, 512, 4], replicated
- loss: float32 [], replicated
All inputs are finite; a program needn't handle non-finite values.
Results may differ from a plain program's by a relative error of at most 0.024.
Values may be sent and summed in bfloat16 or wider, within the bound.
A program may use at most 128 MiB of HBM per device.

v0:
```python
import jax
import jax.numpy as jnp
from jax import lax
from jax.sharding import PartitionSpec as P

HEAD_DIM = 64


latent_scale = 0.18215
norm_eps = 1e-06
cosine_eps = 1e-06


def extended(cells, sides, width):
    for axis, dim in sides:
        count = lax.axis_size(axis)
        ends = count - 1
        head = lax.slice_in_dim(cells, 0, width, axis=dim)
        tail = lax.slice_in_dim(cells, cells.shape[dim] - width, cells.shape[dim], axis=dim)
        cells = jnp.concatenate(
            [
                lax.ppermute(tail, axis, [(i, (i + 1) % count) for i in range(ends)]),
                cells,
                lax.ppermute(head, axis, [((i + 1) % count, i) for i in range(ends)]),
            ],
            axis=dim,
        )
    return cells


def conv_out(padded, conv_w):
    rows = padded.shape[0] - 2
    cols = padded.shape[1] - 2
    total = jnp.zeros((rows * cols, conv_w.shape[2]), jnp.float32)
    for tap in range(9):
        view = padded[tap // 3 : tap // 3 + rows, tap % 3 : tap % 3 + cols]
        total = total + jnp.dot(
            view.reshape(rows * cols, -1), conv_w[tap], preferred_element_type=jnp.float32
        )
    return total.reshape(rows, cols, -1) * latent_scale


def contract_first(left, right):
    return lax.dot_general(
        left, right, (((0,), (0,)), ((), ())), preferred_element_type=jnp.float32
    )


def contract_last(left, right):
    return lax.dot_general(
        left, right, (((1,), (1,)), ((), ())), preferred_element_type=jnp.float32
    )


def conv_back(padded, grad_pad, conv_w):
    rows = grad_pad.shape[0] - 2
    cols = grad_pad.shape[1] - 2
    center = grad_pad[1:-1, 1:-1].reshape(rows * cols, -1)
    grad_in = jnp.zeros((rows * cols, conv_w.shape[1]), jnp.float32)
    parts = []
    for tap in range(9):
        row_off = tap // 3
        col_off = tap % 3
        g_view = grad_pad[
            2 - row_off : 2 - row_off + rows, 2 - col_off : 2 - col_off + cols
        ].reshape(rows * cols, -1)
        grad_in = grad_in + contract_last(g_view, conv_w[tap])
        f_view = padded[row_off : row_off + rows, col_off : col_off + cols].reshape(rows * cols, -1)
        parts.append(contract_first(f_view, center))
    return (grad_in.reshape(rows, cols, -1), jnp.stack(parts, 0))


def patchify(latent):
    rows, cols, chans = latent.shape
    blocks = latent.reshape(rows // 2, 2, cols // 2, 2, chans).transpose(0, 2, 1, 3, 4)
    return blocks.reshape(rows // 2 * (cols // 2), 4 * chans)


def unpatchify(tokens, rows, cols):
    chans = tokens.shape[1] // 4
    blocks = tokens.reshape(rows // 2, cols // 2, 2, 2, chans).transpose(0, 2, 1, 3, 4)
    return blocks.reshape(rows, cols, chans)


def cosine_grad(projected, target):
    norm_p = jnp.sqrt(jnp.sum(projected * projected, -1, keepdims=True) + cosine_eps)
    norm_t = jnp.sqrt(jnp.sum(target * target, -1, keepdims=True) + cosine_eps)
    cosine = jnp.sum(projected * target, -1, keepdims=True) / (norm_p * norm_t)
    grad = cosine * projected / (norm_p * norm_p) - target / (norm_p * norm_t)
    return (cosine[:, 0], grad)


def local(feats, labels, conv_w, embed_w, mod_table, qkv_w, out_w, proj_w, dino):
    image = feats[0]
    rows, cols, chans = image.shape
    width = qkv_w.shape[0]
    heads = width // HEAD_DIM
    scale = HEAD_DIM ** (-0.5)
    rimmed = extended(image, (("slab", 0),), 1)
    padded = jnp.pad(rimmed, ((0, 0), (1, 1), (0, 0)))
    tokens = patchify(conv_out(padded, conv_w))
    count = tokens.shape[0]
    embed_f = embed_w.astype(jnp.float32)
    start = jnp.dot(tokens, embed_f, precision=lax.Precision.HIGHEST)
    row = lax.dynamic_index_in_dim(mod_table, labels[0], 0, keepdims=False).astype(jnp.float32)
    mean = jnp.mean(start, -1, keepdims=True)
    cent = start - mean
    inv = lax.rsqrt(jnp.mean(cent * cent, -1, keepdims=True) + norm_eps)
    normed = cent * inv
    modded = (normed * (1.0 + row[width:]) + row[:width]).astype(jnp.bfloat16)
    qkv = jnp.dot(modded, qkv_w, preferred_element_type=jnp.float32).astype(jnp.bfloat16)
    query = qkv[:, :width]
    key = qkv[:, width : 2 * width]
    value = qkv[:, 2 * width :]
    key_all, value_all = (
        lax.all_gather(key, "slab", axis=0, tiled=True),
        lax.all_gather(value, "slab", axis=0, tiled=True),
    )
    q3 = query.reshape(count, heads, HEAD_DIM)
    k3 = key_all.reshape(-1, heads, HEAD_DIM)
    v3 = value_all.reshape(-1, heads, HEAD_DIM)
    scores = jnp.einsum("qhd,khd->hqk", q3, k3, preferred_element_type=jnp.float32) * scale
    top = jnp.max(scores, -1, keepdims=True)
    expo = jnp.exp(scores - top)
    total = jnp.sum(expo, -1)
    attended = (
        jnp.einsum(
            "hqk,khd->qhd", expo.astype(jnp.bfloat16), v3, preferred_element_type=jnp.float32
        )
        / total.T[:, :, None]
    )
    attended = attended.reshape(count, width).astype(jnp.bfloat16)
    lse = top[..., 0] + jnp.log(total)
    resid = start + jnp.dot(attended, out_w, preferred_element_type=jnp.float32)
    resid_b = resid.astype(jnp.bfloat16)
    projected = jnp.dot(resid_b, proj_w, preferred_element_type=jnp.float32)
    cosine, grad_p = cosine_grad(projected, dino[0].astype(jnp.float32))
    grad_pb = grad_p.astype(jnp.bfloat16)
    proj_part = contract_first(resid_b, grad_pb)
    grad_resid = contract_last(grad_pb, proj_w)
    grad_att = contract_last(grad_resid.astype(jnp.bfloat16), out_w).astype(jnp.bfloat16)
    g3 = grad_att.reshape(count, heads, HEAD_DIM)
    delta = jnp.sum(
        g3.astype(jnp.float32) * attended.reshape(count, heads, HEAD_DIM).astype(jnp.float32), -1
    ).T
    probs = jnp.exp(scores - lse[..., None])
    dprobs = jnp.einsum("qhd,khd->hqk", g3, v3, preferred_element_type=jnp.float32)
    dscores = (probs * (dprobs - delta[..., None])).astype(jnp.bfloat16)
    grad_query = scale * jnp.einsum(
        "hqk,khd->qhd", dscores, k3, preferred_element_type=jnp.float32
    ).reshape(count, width)
    key_terms = scale * jnp.einsum(
        "hqk,qhd->khd", dscores, q3, preferred_element_type=jnp.float32
    ).reshape(-1, width)
    value_terms = jnp.einsum(
        "hqk,qhd->khd", probs.astype(jnp.bfloat16), g3, preferred_element_type=jnp.float32
    ).reshape(-1, width)
    grad_key, grad_value = (
        lax.psum_scatter(
            key_terms.astype(jnp.bfloat16), "slab", scatter_dimension=0, tiled=True
        ).astype(jnp.float32),
        lax.psum_scatter(
            value_terms.astype(jnp.bfloat16), "slab", scatter_dimension=0, tiled=True
        ).astype(jnp.float32),
    )
    grad_qkv = jnp.concatenate([grad_query, grad_key, grad_value], 1).astype(jnp.bfloat16)
    grad_mod = contract_last(grad_qkv, qkv_w)
    grad_norm = grad_mod * (1.0 + row[width:])
    grad_start = grad_resid + inv * (
        grad_norm
        - jnp.mean(grad_norm, -1, keepdims=True)
        - normed * jnp.mean(grad_norm * normed, -1, keepdims=True)
    )
    grad_tokens = jnp.dot(grad_start, embed_f.T, precision=lax.Precision.HIGHEST)
    grad_latent = (unpatchify(grad_tokens, rows, cols) * latent_scale).astype(jnp.bfloat16)
    grad_rim = extended(grad_latent, (("slab", 0),), 1)
    grad_pad = jnp.pad(grad_rim, ((0, 0), (1, 1), (0, 0)))
    grad_image, conv_part = conv_back(padded, grad_pad, conv_w)
    loss_part = jnp.sum(1.0 - cosine)
    grad_proj, grad_conv, loss_sum = lax.psum((proj_part, conv_part, loss_part), ("slab", "img"))
    groups = lax.axis_size("slab") * lax.axis_size("img")
    return (
        grad_image.astype(jnp.bfloat16)[None],
        grad_proj,
        grad_conv,
        loss_sum / (groups * count),
    )


def solution(mesh):
    in_specs = (
        P("img", "slab", None, None),
        P("img"),
        P(),
        P(),
        P(),
        P(),
        P(),
        P(),
        P("img", "slab", None),
    )
    out_specs = (P("img", "slab", None, None), P(), P(), P())
    return jax.shard_map(local, mesh=mesh, in_specs=in_specs, out_specs=out_specs, check_vma=False)
```

profile of v0, /device:TPU:0, one launch (start us, length us, event | category | flops | bytes accessed | tf_op | source)
XLA Modules:
  0.0 356.8 jit_solution(18336326718904891435)
XLA Ops:
  7.2 1.1 slice_bitcast_fusion.1
  8.4 2.4 collective-permute-start
  10.8 1.3 collective-permute-start.1
  12.7 1.6 fusion.113
  14.3 0.8 dynamic-slice_convert_fusion
  15.1 0.6 slice_add_fusion
  16.4 0.6 copy-done.18
  17.0 1.7 fusion.25
  18.7 0.8 fusion.162
  22.4 1.0 fusion.45
  23.4 1.7 copy.45
  25.2 1.9 copy.46
  27.0 0.8 reshape.205
  27.9 1.5 fusion.164
  29.6 4.8 %convolution_convert_fusion = bf16[256,3072]{1,0:T(8,128)(2,1)S(1)} fusion(bf16[1024,3072]{1,0:T(8,128)(2,1)} %param.14, f32[256,1024]{1,0:T(8,128)S(1)} %get-tuple-element.33, f32[1024]{0:T(1024)} %bitcast.264, f32[1024]{0:T(1024)S(1)} %bitcast.262, f32[256]{0:T(256)S(1)} %add_rsqrt_fusion, f32[256]{0:T(256)S(1)} %broadcast_multiply_fusion.2), kind=kOutput, calls=%fused_computation.16 | convolution fusion | flops 1612709888 | bytes 8923136 | tf_op jit(solution)/shard_map/dot_general | solution.py:111
  34.4 1.2 fusion.161
  35.7 0.7 all-gather.3.cloned.1.call-update
  36.4 2.0 copy.48
  38.5 24.5 %all-gather.5.cloned.1.call-done = bf16[1024,1024]{1,0:T(8,128)(2,1)} async-done(((bf16[256,1024]{1,0:T(8,128)(2,1)}), bf16[1024,1024]{1,0:T(8,128)(2,1)}) %all-gather.5.cloned.1.call-update) | async-done | bytes 2097168 | tf_op jit(solution)/shard_map/all_gather | solution.py:116
  63.0 4.0 %copy.49 = bf16[1024,1024]{0,1:T(8,128)(2,1)} copy(bf16[1024,1024]{1,0:T(8,128)(2,1)} %all-gather.5.cloned.1.call-done) | data formatting | bytes 4194304 | tf_op jit(solution)/shard_map/all_gather | solution.py:116
  66.9 4.2 %multiply_reduce_fusion = (f32[16,256]{1,0:T(8,128)S(1)}, f32[16,256,1024]{2,1,0:T(8,128)S(1)}) fusion(bf16[256,16,64]{0,2,1:T(8,128)(2,1)} %bitcast.234, bf16[1024,16,64]{0,2,1:T(8,128)(2,1)} %bitcast.226), kind=kOutput, calls=%fused_computation.6 | convolution fusion | flops 545255424 | bytes 19415040 | tf_op jit(solution)/shard_map/qhd,khd->hqk/dot_general | solution.py:122
  71.2 3.6 %fusion = f32[16,256]{1,0:T(8,128)S(1)} fusion(f32[16,256,1024]{2,1,0:T(8,128)S(1)} %get-tuple-element.35, f32[16,256]{1,0:T(8,128)S(1)} %get-tuple-element.34), kind=kLoop, calls=%fused_computation.3 | loop fusion | flops 12578816 | bytes 16809984 | tf_op jit(solution)/shard_map/reduce_sum | solution.py:125
  74.8 2.3 copy-done.2
  77.3 0.6 copy-done.29
  77.9 9.2 %all-gather.3.cloned.1.call-done = bf16[1024,1024]{1,0:T(8,128)(2,1)} async-done(((bf16[256,1024]{1,0:T(8,128)(2,1)}), bf16[1024,1024]{1,0:T(8,128)(2,1)}) %all-gather.3.cloned.1.call-update) | async-done | bytes 2097168 | tf_op jit(solution)/shard_map/all_gather | solution.py:117
  87.1 3.9 %copy.47 = bf16[1024,1024]{0,1:T(8,128)(2,1)} copy(bf16[1024,1024]{1,0:T(8,128)(2,1)} %all-gather.3.cloned.1.call-done) | data formatting | bytes 4194304 | tf_op jit(solution)/shard_map/all_gather | solution.py:117
  91.0 8.3 %divide_convert_fusion = bf16[256,16,64]{0,2,1:T(8,128)(2,1)S(1)} fusion(bf16[1024,16,64]{0,2,1:T(8,128)(2,1)} %bitcast.231, f32[16,256,1024]{2,1,0:T(8,128)} %copy-done.2, f32[16,256]{1,0:T(8,128)} %copy-done.25, f32[256,16]{0,1:T(8,128)} %bitcast.261), kind=kOutput, calls=%fused_computation.83 | convolution fusion | flops 549978112 | bytes 19431424 | tf_op jit(solution)/shard_map/hqk,khd->qhd/dot_general | solution.py:127
  99.4 0.7 fusion.32
  100.1 0.8 copy-done.17
  101.0 0.7 fusion.73
  101.7 0.6 subtract_reduce_fusion
  102.6 0.8 copy-done.14
  103.4 0.6 fusion.165
  104.0 1.0 copy-done.10
  104.9 1.6 convolution_convert_fusion.1
  106.6 1.2 copy.50
  107.8 1.2 multiply_reduce_fusion.2
  109.0 9.4 %multiply_convert_fusion = bf16[16,256,1024]{2,1,0:T(8,128)(2,1)S(1)} fusion(f32[16,256,1024]{2,1,0:T(8,128)} %copy-done.2, bf16[256,16,64]{0,2,1:T(8,128)(2,1)S(1)} %bitcast.229, bf16[1024,16,64]{0,2,1:T(8,128)(2,1)} %bitcast.232, f32[16,256]{1,0:T(8,128)S(1)} %bitcast.260, f32[16,256]{1,0:T(8,128)S(1)} %log_add_fusion), kind=kOutput, calls=%fused_computation | convolution fusion | flops 557842432 | bytes 27820032 | tf_op jit(solution)/shard_map/qhd,khd->hqk/dot_general | solution.py:147
  118.5 3.4 multiply_convert_fusion.1
  121.9 0.5 copy-done.3
  122.4 9.8 %fusion.12 = bf16[16,64,1024]{2,1,0:T(8,128)(2,1)} fusion(bf16[256,16,64]{0,2,1:T(8,128)(2,1)S(1)} %bitcast.230, f32[16,256,1024]{2,1,0:T(8,128)} %copy-done.2, f32[16,256]{1,0:T(8,128)S(1)} %log_add_fusion), kind=kOutput, calls=%fused_computation.19 | convolution fusion | flops 550502400 | bytes 19415040 | tf_op jit(solution)/shard_map/hqk,qhd->khd/dot_general | solution.py:155
  132.3 39.7 %psum.23 = f32[]{:T(128)} all-reduce(f32[]{:T(128)} %get-tuple-element.11), channel_id=1, replica_groups=mesh['slab'=4,'img'=8] {'slab','img'}, use_global_device_ids=true, to_apply=%region_15.16 | all-reduce | flops 1 | bytes 8 | tf_op jit(solution)/shard_map/psum | solution.py:180
  172.7 3.5 fusion.166
  176.3 6.9 %fusion.33 = bf16[16,64,256]{2,1,0:T(8,128)(2,1)} fusion(bf16[1024,16,64]{0,2,1:T(8,128)(2,1)S(1)} %bitcast.227, bf16[16,256,1024]{2,1,0:T(8,128)(2,1)} %copy-done.3), kind=kOutput, calls=%fused_computation.37 | convolution fusion | flops 537395200 | bytes 11010048 | tf_op jit(solution)/shard_map/hqk,khd->qhd/dot_general | solution.py:149
  183.1 4.4 %reduce-scatter.5.cloned.1.call-done = bf16[256,1024]{0,1:T(8,128)(2,1)} async-done(((bf16[1024,1024]{0,1:T(8,128)(2,1)}), bf16[256,1024]{0,1:T(8,128)(2,1)}) %reduce-scatter.5.cloned.1.call-update) | async-done | bytes 524304 | tf_op jit(solution)/shard_map/reduce_scatter | solution.py:162
  187.5 5.7 %fusion.160 = (f32[256]{0:T(256)S(1)}, f32[256]{0:T(256)S(1)}, f32[256,1024]{1,0:T(8,128)S(1)}) fusion(f32[256]{0:T(256)S(1)} %add_rsqrt_fusion, f32[256,1024]{1,0:T(8,128)} %copy-done.7, f32[256]{0:T(256)S(1)} %broadcast_multiply_fusion.2, f32[1024]{0:T(1024)S(1)} %bitcast.263, bf16[1024,3072]{1,0:T(8,128)(2,1)} %param.14, ...), kind=kOutput, calls=%fused_computation.197 | convolution fusion | flops 1616903680 | bytes 9969664 | tf_op jit(solution)/shard_map/dot_general | solution.py:50
  193.2 0.9 fusion.46
  194.8 1.2 fusion.56
  197.6 1.3 collective-permute-start.3
  199.0 3.3 collective-permute-start.2
  202.3 1.8 fusion.111
  204.9 0.5 copy-done.27
  205.7 0.5 fusion.87
  206.2 0.5 fusion.91
  206.7 0.5 fusion.92
  207.2 0.5 fusion.96
  207.7 0.5 fusion.93
  208.2 0.5 fusion.94
  208.7 0.5 fusion.99
  209.3 0.5 copy-done.12
  209.8 2.1 add_convert_fusion
  211.9 132.6 %all-reduce.5.cloned.1.call-done = (f32[1024,768]{1,0:T(8,128)}, f32[9,512,4]{1,2,0:T(4,128)}) async-done(((f32[1024,768]{1,0:T(8,128)}, f32[9,512,4]{1,2,0:T(4,128)}), (f32[1024,768]{1,0:T(8,128)}, f32[9,512,4]{1,2,0:T(4,128)})) %all-reduce.5.cloned.1.call-update) | async-done | bytes 3219472 | tf_op jit(solution)/shard_map/psum | solution.py:180
  344.6 3.9 %copy.88 = f32[1024,768]{1,0:T(8,128)} copy(f32[1024,768]{1,0:T(8,128)} %get-tuple-element.41) | data formatting | bytes 6291456
  348.5 0.6 copy.89
  (94 shorter events, 8.0 us)
Async XLA Ops:
  7.2 92.2 %copy-start = (bf16[1024,1024]{1,0:T(8,128)(2,1)S(1)}, bf16[1024,1024]{1,0:T(8,128)(2,1)}, u32[]{:S(2)}) copy-start(bf16[1024,1024]{1,0:T(8,128)(2,1)} %param.15) | copy-start | bytes 6291460
  7.2 55.8 %all-gather.5.cloned.1.call-start = ((), (), s32[]{:S(2)}) async-start(), calls=%async_computation.3 | async-start | bytes 2621440 | tf_op jit(solution)/shard_map/all_gather | solution.py:116
  8.4 7.3 %collective-permute-start = (bf16[1,128,512]{2,1,0:T(8,128)(2,1)S(1)}, bf16[1,128,512]{2,1,0:T(8,128)(2,1)S(1)}, u32[]{:S(2)}, u32[]{:S(2)}) collective-permute-start(bf16[1,128,512]{2,1,0:T(8,128)(2,1)S(1)} %get-tuple-element.25), channel_id=1, source_target_pairs={{0,8},{8,16},{16,24},{1,9},{9,17},{17,25},{2,10},{10,18},{18,26},{... | collective-permute-start | bytes 393224 | tf_op jit(solution)/shard_map/ppermute | solution.py:22
  10.8 5.3 %collective-permute-start.1 = (bf16[1,128,512]{2,1,0:T(8,128)(2,1)S(1)}, bf16[1,128,512]{2,1,0:T(8,128)(2,1)S(1)}, u32[]{:S(2)}, u32[]{:S(2)}) collective-permute-start(bf16[1,128,512]{2,1,0:T(8,128)(2,1)S(1)} %get-tuple-element.26), channel_id=1, source_target_pairs={{8,0},{16,8},{24,16},{9,1},{17,9},{25,17},{10,2},{18,10},{26,18},{... | collective-permute-start | bytes 393224 | tf_op jit(solution)/shard_map/ppermute | solution.py:24
  15.7 0.7 copy-start.21
  16.4 0.6 copy-start.18
  18.7 0.9 copy-start.24
  19.9 1.5 copy-start.4
  19.9 1.5 copy-start.19
  19.9 1.6 copy-start.22
  29.3 5.1 %copy-start.7 = (f32[256,1024]{1,0:T(8,128)}, f32[256,1024]{1,0:T(8,128)S(1)}, u32[]{:S(2)}) copy-start(f32[256,1024]{1,0:T(8,128)S(1)} %get-tuple-element.33) | copy-start | bytes 3145732
  35.6 51.5 %all-gather.3.cloned.1.call-start = ((), (), s32[]{:S(2)}) async-start(), calls=%async_computation.2 | async-start | bytes 2621440 | tf_op jit(solution)/shard_map/all_gather | solution.py:117
  36.4 146.7 %reduce-scatter.3.cloned.1.call-start = ((), (), s32[]{:S(2)}) async-start(), calls=%async_computation.4 | async-start | bytes 2621440 | tf_op jit(solution)/shard_map/reduce_scatter | solution.py:159
  71.1 6.0 %copy-start.2 = (f32[16,256,1024]{2,1,0:T(8,128)}, f32[16,256,1024]{2,1,0:T(8,128)S(1)}, u32[]{:S(2)}) copy-start(f32[16,256,1024]{2,1,0:T(8,128)S(1)} %get-tuple-element.35) | copy-start | bytes 50331652
  71.1 6.1 %copy-start.25 = (f32[16,256]{1,0:T(8,128)}, f32[16,256]{1,0:T(8,128)S(1)}, u32[]{:S(2)}) copy-start(f32[16,256]{1,0:T(8,128)S(1)} %get-tuple-element.34) | copy-start | bytes 49156
  77.3 0.6 copy-start.29
  91.0 8.3 %copy-start.8 = (f32[256,1024]{1,0:T(8,128)S(1)}, f32[256,1024]{1,0:T(8,128)}, u32[]{:S(2)}) copy-start(f32[256,1024]{1,0:T(8,128)} %copy-done.7) | copy-start | bytes 3145732
  99.3 0.8 copy-start.15
  99.4 1.6 copy-start.17
  99.4 1.6 copy-start.23
  101.0 1.4 copy-start.16
  102.6 0.8 copy-start.14
  104.0 1.0 copy-start.10
  109.0 9.5 %copy-start.13 = (bf16[256,1024]{0,1:T(8,128)(2,1)S(1)}, bf16[256,1024]{0,1:T(8,128)(2,1)}, u32[]{:S(2)}) copy-start(bf16[256,1024]{0,1:T(8,128)(2,1)} %copy.48) | copy-start | bytes 1572868
  118.5 3.9 %copy-start.3 = (bf16[16,256,1024]{2,1,0:T(8,128)(2,1)}, bf16[16,256,1024]{2,1,0:T(8,128)(2,1)S(1)}, u32[]{:S(2)}) copy-start(bf16[16,256,1024]{2,1,0:T(8,128)(2,1)S(1)} %multiply_convert_fusion) | copy-start | bytes 25165828
  122.4 65.1 %reduce-scatter.5.cloned.1.call-start = ((), (), s32[]{:S(2)}) async-start(), calls=%async_computation.5 | async-start | bytes 2621440 | tf_op jit(solution)/shard_map/reduce_scatter | solution.py:162
  132.3 44.0 %copy-start.6 = (bf16[1024,1024]{0,1:T(8,128)(2,1)S(1)}, bf16[1024,1024]{0,1:T(8,128)(2,1)}, u32[]{:S(2)}) copy-start(bf16[1024,1024]{0,1:T(8,128)(2,1)} %copy.49) | copy-start | bytes 6291460
  132.3 212.3 %all-reduce.5.cloned.1.call-start = ((), (), s32[]{:S(2)}) async-start(), calls=%async_computation.6 | async-start | bytes 6438912 | tf_op jit(solution)/shard_map/psum | solution.py:180
  187.5 5.7 %copy-start.9 = (f32[256,1024]{1,0:T(8,128)S(1)}, f32[256,1024]{1,0:T(8,128)}, u32[]{:S(2)}) copy-start(f32[256,1024]{1,0:T(8,128)} %copy-done.7) | copy-start | bytes 3145732
  187.5 5.7 %copy-start.11 = (f32[256,1024]{1,0:T(8,128)S(1)}, f32[256,1024]{1,0:T(8,128)}, u32[]{:S(2)}) copy-start(f32[256,1024]{1,0:T(8,128)} %copy-done.10) | copy-start | bytes 3145732
  187.5 5.7 %copy-start.26 = (bf16[16,1024]{1,0:T(8,128)(2,1)S(1)}, bf16[16,1024]{1,0:T(8,128)(2,1)}, u32[]{:S(2)}) copy-start(bf16[16,1024]{1,0:T(8,128)(2,1)} %param.12) | copy-start | bytes 98308
  193.2 1.6 copy-start.5
  197.4 6.7 %copy-start.20 = (bf16[1,128,512]{2,1,0:T(8,128)(2,1)S(1)}, bf16[1,128,512]{2,1,0:T(8,128)(2,1)}, u32[]{:S(2)}) copy-start(bf16[1,128,512]{2,1,0:T(8,128)(2,1)} %copy-done.18) | copy-start | bytes 393220
  197.6 7.7 %collective-permute-start.3 = (bf16[1,128,4]{2,1,0:T(8,128)(2,1)S(1)}, bf16[1,128,4]{2,1,0:T(8,128)(2,1)S(1)}, u32[]{:S(2)}, u32[]{:S(2)}) collective-permute-start(bf16[1,128,4]{2,1,0:T(8,128)(2,1)S(1)} %get-tuple-element.28), channel_id=1, source_target_pairs={{8,0},{16,8},{24,16},{9,1},{17,9},{25,17},{10,2},{18,10},{26,18},{... | collective-permute-start | bytes 3080 | tf_op jit(solution)/shard_map/ppermute | solution.py:24
  199.0 6.5 %collective-permute-start.2 = (bf16[1,128,4]{2,1,0:T(8,128)(2,1)S(1)}, bf16[1,128,4]{2,1,0:T(8,128)(2,1)S(1)}, u32[]{:S(2)}, u32[]{:S(2)}) collective-permute-start(bf16[1,128,4]{2,1,0:T(8,128)(2,1)S(1)} %get-tuple-element.27), channel_id=1, source_target_pairs={{0,8},{8,16},{16,24},{1,9},{9,17},{17,25},{2,10},{10,18},{18,26},{... | collective-permute-start | bytes 3080 | tf_op jit(solution)/shard_map/ppermute | solution.py:22
  204.7 0.6 copy-start.27
  208.2 1.6 copy-start.12
  344.6 4.6 %copy-start.1 = (bf16[1024,1024]{1,0:T(8,128)(2,1)S(1)}, bf16[1024,1024]{1,0:T(8,128)(2,1)}, u32[]{:S(2)}) copy-start(bf16[1024,1024]{1,0:T(8,128)(2,1)} %param.15) | copy-start | bytes 6291460
  344.6 3.9 %copy-start.28 = (f32[9,512,4]{1,2,0:T(4,128)S(1)}, f32[9,512,4]{1,2,0:T(4,128)}, u32[]{:S(2)}) copy-start(f32[9,512,4]{1,2,0:T(4,128)} %get-tuple-element.42) | copy-start | bytes 221188
Sparse Core Ops, SparseCore 0:
  35.8 27.1 all-gather.4
  64.5 22.5 all-gather.2
  122.5 31.3 reduce-scatter.2
  156.3 31.1 reduce-scatter.4
  205.5 139.0 all-reduce.4
where the time goes:
time: 358 us; the launch traced here: 357 us
  waiting for transfers between devices  172 us (48%)
  matrix products  78.6 us (22%)
  blocking collectives  39.7 us (11%)
  local copies, waits for them, and re-layouts  32.2 us (9%)
  between operations  16.7 us (5%)
  other arithmetic  9.29 us (3%)
  starting transfers between devices  8.48 us (2%)
    psum x1, waiting for transfers between devices, local(): lax.psum((proj_part, conv_part, loss_part), ('slab', 'img'))  133 us
    psum x1, blocking collectives, local(): lax.psum((proj_part, conv_part, loss_part), ('slab', 'img'))  39.7 us
    all_gather x1, waiting for transfers between devices, local(): lax.all_gather(key, 'slab', axis=0, tiled=True)  24.5 us
    dot_general x12, matrix products, contract_last(): lax.dot_general(left, right, (((1,), (1,)), ((), ())), preferred_element_...  15.3 us
    unnamed x62, local copies, waits for them, and re-layouts  12.8 us
    dot_general x1, matrix products, local(): jnp.einsum('hqk,qhd->khd', probs.astype(jnp.bfloat16), g3, preferred_elem...  9.81 us
    dot_general x1, matrix products, local(): jnp.einsum('qhd,khd->hqk', g3, v3, preferred_element_type=jnp.float32)  9.44 us
    all_gather x1, waiting for transfers between devices, local(): lax.all_gather(value, 'slab', axis=0, tiled=True)  9.23 us
  transfers between devices with their start and end apart: 9, of which 5 were waited for; matrix products, arithmetic and copies ran while one was open for 13% of the time, Pallas kernels for 0%

commit v1 on v0

v1 whole, which is shorter than its diff:
```python
import functools
import math

import jax
import jax.numpy as jnp
from jax import lax
from jax.experimental import pallas as pl
from jax.experimental.pallas import tpu as pltpu
from jax.sharding import PartitionSpec as P

HEAD_DIM = 64
PAIR = 2 * HEAD_DIM

latent_scale = 0.18215
norm_eps = 1e-06
cosine_eps = 1e-06

MESH_ID = pl.DeviceIdType.MESH


def mm(left, right, dims, kind=jnp.float32):
    return lax.dot_general(left, right, (dims, ((), ())), preferred_element_type=kind)


def contract_first(left, right):
    return mm(left, right, ((0,), (0,)))


def contract_last(left, right):
    return mm(left, right, ((1,), (1,)))


def attend_kernel(q_ref, k_ref, v_ref, o_ref, lse_ref):
    scale = HEAD_DIM ** (-0.5)
    outs = []
    for h in range(2):
        cut = slice(h * HEAD_DIM, (h + 1) * HEAD_DIM)
        s = contract_last(k_ref[:, cut], q_ref[:, cut] * jnp.bfloat16(scale))
        top = jnp.max(s, 0, keepdims=True)
        e = jnp.exp(s - top)
        total = jnp.sum(e, 0, keepdims=True)
        o = contract_first(v_ref[:, cut], e.astype(jnp.bfloat16)) / total
        lse_ref[0, h : h + 1, :] = top + jnp.log(total)
        outs.append(o)
    o_ref[...] = jnp.concatenate(outs, 0).T.astype(jnp.bfloat16)


def attend_back_kernel(q_ref, k_ref, v_ref, g_ref, o_ref, lse_ref, gq_ref, gk_ref, gv_ref):
    scale = HEAD_DIM ** (-0.5)
    prod = (g_ref[...].astype(jnp.float32) * o_ref[...].astype(jnp.float32)).T
    gqs = []
    for h in range(2):
        cut = slice(h * HEAD_DIM, (h + 1) * HEAD_DIM)
        qs = q_ref[:, cut] * jnp.bfloat16(scale)
        k = k_ref[:, cut]
        g = g_ref[:, cut]
        delta = jnp.sum(prod[cut], 0, keepdims=True)
        p = jnp.exp(contract_last(k, qs) - lse_ref[0, h : h + 1, :])
        ds = (p * (contract_last(v_ref[:, cut], g) - delta)).astype(jnp.bfloat16)
        gk_ref[:, cut] = mm(ds, qs, ((1,), (0,))).astype(jnp.bfloat16)
        gv_ref[:, cut] = mm(p.astype(jnp.bfloat16), g, ((1,), (0,))).astype(jnp.bfloat16)
        gqs.append(contract_first(k, ds) * scale)
    gq_ref[...] = jnp.concatenate(gqs, 0).T.astype(jnp.bfloat16)


def attend(query, kv):
    count, width = query.shape
    full = kv.shape[0]
    pairs = width // PAIR
    cost = pl.CostEstimate(
        flops=4 * count * full * width, bytes_accessed=2 * (2 * full + 2 * count) * width,
        transcendentals=count * full * width // HEAD_DIM)
    return pl.pallas_call(
        attend_kernel,
        grid=(pairs,),
        in_specs=[
            pl.BlockSpec((count, PAIR), lambda i: (0, i)),
            pl.BlockSpec((full, PAIR), lambda i: (0, i)),
            pl.BlockSpec((full, PAIR), lambda i: (0, i + pairs)),
        ],
        out_specs=[
            pl.BlockSpec((count, PAIR), lambda i: (0, i)),
            pl.BlockSpec((1, 2, count), lambda i: (i, 0, 0)),
        ],
        out_shape=[
            jax.ShapeDtypeStruct((count, width), jnp.bfloat16),
            jax.ShapeDtypeStruct((pairs, 2, count), jnp.float32),
        ],
        cost_estimate=cost,
        name="attend",
    )(query, kv, kv)


def attend_back(query, kv, grad, attended, lse):
    count, width = query.shape
    full = kv.shape[0]
    pairs = width // PAIR
    cost = pl.CostEstimate(
        flops=10 * count * full * width, bytes_accessed=2 * (4 * full + 4 * count) * width,
        transcendentals=count * full * width // HEAD_DIM)
    small = pl.BlockSpec((count, PAIR), lambda i: (0, i))
    large = pl.BlockSpec((full, PAIR), lambda i: (0, i))
    return pl.pallas_call(
        attend_back_kernel,
        grid=(pairs,),
        in_specs=[
            small,
            large,
            pl.BlockSpec((full, PAIR), lambda i: (0, i + pairs)),
            small,
            small,
            pl.BlockSpec((1, 2, count), lambda i: (i, 0, 0)),
        ],
        out_specs=[small, large, large],
        out_shape=[
            jax.ShapeDtypeStruct((count, width), jnp.bfloat16),
            jax.ShapeDtypeStruct((full, width), jnp.bfloat16),
            jax.ShapeDtypeStruct((full, width), jnp.bfloat16),
        ],
        cost_estimate=cost,
        name="attend_back",
    )(query, kv, kv, grad, attended, lse)


def reduce_kernel(slabs, images, x_ref, out_ref, recv, send1, recv1, send2, recv2):
    count = slabs * images
    me = lax.axis_index("slab") * images + lax.axis_index("img")

    def where(step):
        peer = lax.rem(me + step, count)
        return peer, {"slab": peer // images, "img": lax.rem(peer, images)}

    barrier = pltpu.get_barrier_semaphore()

    def hello(step, _):
        _, spot = where(step)
        pl.semaphore_signal(barrier, inc=1, device_id=spot, device_id_type=MESH_ID)
        return 0

    lax.fori_loop(1, count, hello, 0)
    pl.semaphore_wait(barrier, count - 1)

    def spread(step):
        peer, spot = where(step)
        return pltpu.make_async_remote_copy(
            src_ref=x_ref.at[peer], dst_ref=recv.at[me], send_sem=send1.at[peer],
            recv_sem=recv1.at[me], device_id=spot, device_id_type=MESH_ID)

    def arrive(step):
        peer, spot = where(step)
        return pltpu.make_async_remote_copy(
            src_ref=x_ref.at[peer], dst_ref=recv.at[peer], send_sem=send1.at[peer],
            recv_sem=recv1.at[peer], device_id=spot, device_id_type=MESH_ID)

    def share(step):
        peer, spot = where(step)
        return pltpu.make_async_remote_copy(
            src_ref=out_ref.at[me], dst_ref=out_ref.at[me], send_sem=send2.at[peer],
            recv_sem=recv2.at[me], device_id=spot, device_id_type=MESH_ID)

    def landed(step):
        peer, spot = where(step)
        return pltpu.make_async_remote_copy(
            src_ref=out_ref.at[me], dst_ref=out_ref.at[peer], send_sem=send2.at[peer],
            recv_sem=recv2.at[peer], device_id=spot, device_id_type=MESH_ID)

    def each(body):
        def run(step, _):
            body(step)
            return 0

        lax.fori_loop(1, count, run, 0)

    each(lambda step: spread(step).start())
    each(lambda step: arrive(step).wait_recv())
    total = x_ref[me]
    total = lax.fori_loop(
        1, count, lambda step, acc: acc + recv[lax.rem(me + step, count)], total)
    out_ref[me] = total
    each(lambda step: share(step).start())
    each(lambda step: spread(step).wait_send())
    each(lambda step: landed(step).wait_recv())
    each(lambda step: share(step).wait_send())


def reduce_small(flat, slabs, images):
    count = slabs * images
    rows = math.ceil(flat.size / count / 1024) * 8
    cells = jnp.pad(flat, (0, count * rows * 128 - flat.size)).reshape(count, rows, 128)
    vmem = pl.BlockSpec(memory_space=pltpu.VMEM)
    out = pl.pallas_call(
        functools.partial(reduce_kernel, slabs, images),
        out_shape=jax.ShapeDtypeStruct(cells.shape, cells.dtype),
        in_specs=[vmem],
        out_specs=vmem,
        scratch_shapes=[pltpu.VMEM(cells.shape, cells.dtype)]
        + [pltpu.SemaphoreType.DMA((count,))] * 4,
        compiler_params=pltpu.CompilerParams(collective_id=0, has_side_effects=True),
        name="reduce_small",
    )(cells)
    return out.reshape(-1)[: flat.size]


def cosine_grad(projected, target):
    norm_p = jnp.sqrt(jnp.sum(projected * projected, -1, keepdims=True) + cosine_eps)
    norm_t = jnp.sqrt(jnp.sum(target * target, -1, keepdims=True) + cosine_eps)
    cosine = jnp.sum(projected * target, -1, keepdims=True) / (norm_p * norm_t)
    grad = cosine * projected / (norm_p * norm_p) - target / (norm_p * norm_t)
    return (cosine[:, 0], grad)


def local(feats, labels, conv_w, embed_w, mod_table, qkv_w, out_w, proj_w, dino):
    image = feats[0]
    rows, cols, chans = image.shape
    outs = conv_w.shape[2]
    width = qkv_w.shape[0]
    slabs = lax.axis_size("slab")
    images = lax.axis_size("img")
    slab = lax.axis_index("slab")
    cells = image.reshape(rows * cols, chans)
    taps = conv_w.transpose(0, 2, 1).reshape(9 * outs, chans)
    resp = contract_last(taps, cells).reshape(3, 3, outs, rows, cols)
    resp = jnp.pad(resp, ((0, 0), (0, 0), (0, 0), (0, 0), (1, 1)))
    flat = sum(resp[:, kx, :, :, kx : kx + cols] for kx in range(3))
    terms = sum(
        jnp.pad(flat[ky], ((0, 0), (2 - ky, ky), (0, 0))) for ky in range(3)
    )
    terms_all = lax.all_gather(terms, "slab", axis=0)
    full_rows = rows * slabs
    latent = sum(
        jnp.pad(terms_all[s], ((0, 0), (s * rows, full_rows - (s + 1) * rows), (0, 0)))
        for s in range(slabs)
    )[:, 1:-1] * latent_scale
    tokens = latent.reshape(outs, full_rows // 2, 2, cols // 2, 2).transpose(1, 3, 2, 4, 0)
    tokens = tokens.reshape(-1, 4 * outs)
    full = tokens.shape[0]
    count = full // slabs
    own = slab * count
    high = lax.reduce_precision(tokens, 8, 7)
    mid = lax.reduce_precision(tokens - high, 8, 7)
    low = tokens - high - mid
    split = jnp.concatenate([high, mid, low], 1).astype(jnp.bfloat16)
    start = jnp.dot(
        split, jnp.concatenate([embed_w] * 3, 0), preferred_element_type=jnp.float32
    )
    row = lax.dynamic_index_in_dim(mod_table, labels[0], 0, keepdims=False).astype(jnp.float32)
    gain = 1.0 + row[width:]
    mean = jnp.mean(start, -1, keepdims=True)
    cent = start - mean
    inv = lax.rsqrt(jnp.mean(cent * cent, -1, keepdims=True) + norm_eps)
    normed = cent * inv
    modded = (normed * gain + row[:width]).astype(jnp.bfloat16)

    def mine(whole):
        return lax.dynamic_slice_in_dim(whole, own, count, 0)

    kv = jnp.dot(modded, qkv_w[:, width:], preferred_element_type=jnp.float32).astype(jnp.bfloat16)
    query = jnp.dot(
        mine(modded), qkv_w[:, :width], preferred_element_type=jnp.float32
    ).astype(jnp.bfloat16)
    attended, lse = attend(query, kv)
    resid = mine(start) + jnp.dot(attended, out_w, preferred_element_type=jnp.float32)
    resid_b = resid.astype(jnp.bfloat16)
    projected = jnp.dot(resid_b, proj_w, preferred_element_type=jnp.float32)
    cosine, grad_p = cosine_grad(projected, dino[0].astype(jnp.float32))
    grad_pb = grad_p.astype(jnp.bfloat16)
    proj_part = contract_first(resid_b, grad_pb).astype(jnp.bfloat16)
    grad_proj = lax.psum(proj_part, ("slab", "img")).astype(jnp.float32)
    grad_resid = contract_last(grad_pb, proj_w)
    grad_att = contract_last(grad_resid.astype(jnp.bfloat16), out_w).astype(jnp.bfloat16)
    grad_query, grad_key, grad_value = attend_back(query, kv, grad_att, attended, lse)

    def norm_back(grad_mod, inv, normed):
        grad_norm = grad_mod * gain
        return inv * (
            grad_norm
            - jnp.mean(grad_norm, -1, keepdims=True)
            - normed * jnp.mean(grad_norm * normed, -1, keepdims=True)
        )

    grad_mod = contract_last(grad_key, qkv_w[:, width : 2 * width]) + contract_last(
        grad_value, qkv_w[:, 2 * width :]
    )
    spread = contract_last(embed_w, norm_back(grad_mod, inv, normed).astype(jnp.bfloat16))
    grad_own = grad_resid + norm_back(
        contract_last(grad_query, qkv_w[:, :width]), mine(inv), mine(normed)
    )
    spread_own = contract_last(embed_w, grad_own.astype(jnp.bfloat16))
    spread = spread + lax.dynamic_update_slice_in_dim(
        jnp.zeros_like(spread), spread_own, own, 1
    )
    grad_tokens = lax.psum(spread, "slab")
    grad_latent = grad_tokens.reshape(2, 2, outs, full_rows // 2, cols // 2)
    grad_latent = grad_latent.transpose(2, 3, 0, 4, 1).reshape(outs, full_rows, cols)
    grad_latent = (grad_latent * latent_scale).astype(jnp.bfloat16)
    grad_pad = lax.dynamic_slice_in_dim(
        jnp.pad(grad_latent, ((0, 0), (1, 1), (1, 1))), slab * rows, rows + 2, 1
    )
    views = jnp.concatenate(
        [
            grad_pad[:, 2 - ky : 2 - ky + rows, 2 - kx : 2 - kx + cols]
            for ky in range(3)
            for kx in range(3)
        ],
        0,
    ).reshape(9 * outs, rows * cols)
    grad_image = contract_first(views, taps).astype(jnp.bfloat16).reshape(1, rows, cols, chans)
    conv_part = mm(views, cells, ((1,), (0,)))
    loss_part = jnp.sum(1.0 - cosine)
    summed = reduce_small(
        jnp.concatenate([conv_part.reshape(-1), loss_part[None]]), slabs, images
    )
    grad_conv = summed[:-1].reshape(9, outs, chans).transpose(0, 2, 1)
    return (grad_image, grad_proj, grad_conv, summed[-1] / (slabs * images * count))


def solution(mesh):
    in_specs = (
        P("img", "slab", None, None),
        P("img"),
        P(),
        P(),
        P(),
        P(),
        P(),
        P(),
        P("img", "slab", None),
    )
    out_specs = (P("img", "slab", None, None), P(), P(), P())
    return jax.shard_map(local, mesh=mesh, in_specs=in_specs, out_specs=out_specs, check_vma=False)
```

time: 358 us -> 278 us (0.78)
  Pallas kernels: 0 us -> 49.1 us
  matrix products: 78.6 us -> 36.6 us
  waiting for transfers between devices: 172 us -> 132 us
  blocking collectives: 39.7 us -> 6.51 us
  starting transfers between devices: 8.48 us -> 0.08 us
  local copies, waits for them, and re-layouts: 32.2 us -> 23.9 us
    pallas_call x0 -> x3, Pallas kernels: none -> 49.1 us  [the longest x1 20.2 us: reduce_small(): pl.pallas_call(functools.partial(reduce_kernel, slabs, images), out_shape...]
    dot_general x41 -> x15, matrix products: 77.8 us -> 35.8 us  [the longest x11 21.1 us: mm(): lax.dot_general(left, right, (dims, ((), ())), preferred_element_type=kind)]
    psum x1 -> x0, blocking collectives: 39.7 us -> none  [local(): lax.psum((proj_part, conv_part, loss_part), ('slab', 'img'))]
    all_gather x2 -> x0, waiting for transfers between devices: 33.7 us -> none  [the longest x1 24.5 us: local(): lax.all_gather(key, 'slab', axis=0, tiled=True)]
    unnamed x62 -> x39, local copies, waits for them, and re-layouts: 12.8 us -> 3.01 us
    convert_element_type x0 -> x3, other arithmetic: none -> 8.97 us  [the longest x1 4.82 us: local(): modded = (normed * gain + row[:width]).astype(jnp.bfloat16)]
    slice x5 -> x14, local copies, waits for them, and re-layouts: 5.2 us -> 13.5 us  [the longest x10 10.8 us: local(): grad_pad[:, 2 - ky:2 - ky + rows, 2 - kx:2 - kx + cols]]
    ppermute x4 -> x0, starting transfers between devices: 8.28 us -> none  [the longest x2 5.7 us: extended(): lax.ppermute(tail, axis, [(i, (i + 1) % count) for i in range(ends)])]
  transfers between devices with their start and end apart: 9 -> 2, of which waited for: 5 -> 2; matrix products, arithmetic and copies ran while one was open for 13% -> 8% of each run, Pallas kernels for 0% -> 7%
where the time goes in v1:
time: 278 us; the launch traced here: 277 us
  waiting for transfers between devices  132 us (47%)
  Pallas kernels  49.1 us (18%)
  matrix products  36.6 us (13%)
  local copies, waits for them, and re-layouts  23.9 us (9%)
  between operations  17 us (6%)
  other arithmetic  12.6 us (5%)
  blocking collectives  6.51 us (2%)
    psum x1, waiting for transfers between devices, local(): grad_proj = lax.psum(proj_part, ('slab', 'img')).astype(jnp.float32)  100 us
    psum x1, waiting for transfers between devices, local(): grad_tokens = lax.psum(spread, 'slab')  31.5 us
    dot_general x11, matrix products, mm(): lax.dot_general(left, right, (dims, ((), ())), preferred_element_type=kind)  21.1 us
    pallas_call x1, Pallas kernels, reduce_small(): pl.pallas_call(functools.partial(reduce_kernel, slabs, images), out_shape...  20.2 us
    pallas_call x1, Pallas kernels, attend_back(): pl.pallas_call(attend_back_kernel, grid=(pairs,), in_specs=[small, large,...  14.5 us
    pallas_call x1, Pallas kernels, attend(): pl.pallas_call(attend_kernel, grid=(pairs,), in_specs=[pl.BlockSpec((coun...  14.3 us
    slice x10, local copies, waits for them, and re-layouts, local(): grad_pad[:, 2 - ky:2 - ky + rows, 2 - kx:2 - kx + cols]  10.8 us
    dot_general x1, matrix products, local(): jnp.dot(modded, qkv_w[:, width:], preferred_element_type=jnp.float32)  8.32 us
  transfers between devices with their start and end apart: 2, of which 2 were waited for; matrix products, arithmetic and copies ran while one was open for 8% of the time, Pallas kernels for 7%

profile of v1, /device:TPU:0, one launch (start us, length us, event | category | flops | bytes accessed | tf_op | source)
XLA Modules:
  0.0 277.3 jit_solution(12782932031898007868)
XLA Ops:
  7.2 0.0 copy-start
  7.2 0.0 copy-start.9
  7.2 0.0 all-reduce.13.cloned.1.call-start
  8.0 0.8 dynamic-slice_convert_fusion
  8.8 1.7 fusion.25
  10.5 0.1 fusion.51
  10.6 6.5 %all-gather = f32[16,10,128]{2,1,0:T(8,128)S(1)} all-gather(f32[4,10,128]{2,1,0:T(8,128)S(1)} %copy.22), channel_id=2, replica_groups=mesh['slab'=4,'img'=8] {'slab'}, dimensions={0}, use_global_device_ids=true | all-gather | bytes 102400 | tf_op jit(solution)/shard_map/all_gather | solution.py:228
  17.2 2.0 copy.23
  19.2 2.8 copy.24
  21.9 0.1 reshape.138
  22.1 0.0 copy-done.9
  22.1 0.8 fusion.59
  22.9 2.0 copy-done.2
  24.8 0.5 multiply_reduce_fusion.1
  25.3 4.8 %add_convert_fusion = (bf16[1024,1024]{0,1:T(8,128)(2,1)S(1)}, f32[1024,1024]{0,1:T(8,128)}) fusion(f32[1024]{0:T(1024)S(1)} %bitcast.92, f32[1024]{0:T(1024)S(1)} %bitcast.89, f32[1024]{0:T(1024)S(1)} %add_rsqrt_fusion, f32[1024,1024]{0,1:T(8,128)} %copy-done.2, f32[1024]{0:T(1024)S(1)} %broadcast_multiply_fusion.2), kind=kLoop, calls=%fused_computation.5 | loop fusion | flops 5242880 | bytes 10502144 | tf_op jit(solution)/shard_map/convert_element_type | solution.py:252
  30.1 8.3 %fusion.2.k_ref.v_ref = bf16[1024,2048]{1,0:T(8,128)(2,1)} fusion(bf16[1024,1024]{0,1:T(8,128)(2,1)S(1)} %get-tuple-element.24, bf16[1024,3072]{1,0:T(8,128)(2,1)} %param.14), kind=kOutput, calls=%fused_computation.8 | convolution fusion | flops 4297064448 | bytes 10485760 | tf_op jit(solution)/shard_map/dot_general | solution.py:257
  38.5 3.2 %fusion.19.q_ref = bf16[256,1024]{1,0:T(8,128)(2,1)} fusion(bf16[1024,3072]{1,0:T(8,128)(2,1)} %param.14, bf16[1024,1024]{0,1:T(8,128)(2,1)S(1)} %get-tuple-element.24, s32[]{:T(128)S(6)} %select_n.15), kind=kOutput, calls=%fused_computation.22 | convolution fusion | flops 537133056 | bytes 3145732 | tf_op jit(solution)/shard_map/dot_general | solution.py:258
  41.6 14.3 %attend.1 = (bf16[256,1024]{1,0:T(8,128)(2,1)}, f32[8,2,256]{2,1,0:T(2,128)}) custom-call(bf16[256,1024]{1,0:T(8,128)(2,1)} %fusion.19.q_ref, bf16[1024,2048]{1,0:T(8,128)(2,1)} %fusion.2.k_ref.v_ref, bf16[1024,2048]{1,0:T(8,128)(2,1)} %fusion.2.k_ref.v_ref), custom_call_target="tpu_custom_call" | custom-call | flops 1073741824 | bytes 5242880 | tf_op jit(solution)/shard_map/attend/pallas_call | solution.py:73
  55.9 2.5 fusion.22
  58.4 0.8 fusion.27
  59.2 0.6 subtract_reduce_fusion
  59.9 0.2 fusion.30
  60.1 0.6 fusion.60
  60.7 1.5 convolution_convert_fusion.2.g_ref
  62.2 1.3 copy.27
  63.6 0.1 dynamic-slice.5
  63.6 14.5 %attend_back.1 = (bf16[256,1024]{1,0:T(8,128)(2,1)}, bf16[1024,1024]{1,0:T(8,128)(2,1)}, bf16[1024,1024]{1,0:T(8,128)(2,1)}) custom-call(bf16[256,1024]{1,0:T(8,128)(2,1)} %fusion.19.q_ref, bf16[1024,2048]{1,0:T(8,128)(2,1)} %fusion.2.k_ref.v_ref, bf16[1024,2048]{1,0:T(8,128)(2,1)} %fusion.2.k_ref.v_ref, bf16[256,1024]{1,0:T(8,128)(2,1)} %convolution_convert_fusion.2.g_ref, ...), custom_call_target="tpu_custom_call" | custom-call | flops 2684354560 | bytes 10485760 | tf_op jit(solution)/shard_map/attend_back/pallas_call | solution.py:103
  78.2 0.0 copy-start.4
  78.2 4.7 %fusion.5 = f32[1024,1024]{0,1:T(8,128)S(1)} fusion(bf16[1024,1024]{1,0:T(8,128)(2,1)} %get-tuple-element.12, bf16[1024,3072]{1,0:T(8,128)(2,1)} %param.14), kind=kOutput, calls=%fused_computation.9 | convolution fusion | flops 2147483648 | bytes 8388608 | tf_op jit(solution)/shard_map/dot_general | solution.py:22
  82.9 0.0 copy-start.10
  83.0 4.4 %fusion.56 = (f32[1024]{0:T(1024)S(1)}, f32[1024]{0:T(1024)S(1)}, f32[1024,1024]{0,1:T(8,128)S(1)}) fusion(f32[1024,1024]{0,1:T(8,128)S(1)} %copy-done.1, f32[1024]{0:T(1024)S(1)} %bitcast.90, f32[1024,1024]{0,1:T(8,128)S(1)} %fusion.5, bf16[1024,1024]{1,0:T(8,128)(2,1)S(1)} %copy-done.4, bf16[1024,3072]{1,0:T(8,128)(2,1)} %param.14), kind=kOutput, calls=%fused_computation.110 | convolution fusion | flops 2152724480 | bytes 16789504 | tf_op jit(solution)/shard_map/dot_general | solution.py:22
  87.4 0.8 fusion.9
  88.1 0.3 copy-done.13
  88.4 2.4 fusion.57
  90.8 0.0 copy-start.12
  90.9 0.4 fusion.24
  91.2 0.6 copy-done.11
  91.9 0.0 all-reduce.13.cloned.1.call-update
  91.9 0.0 all-reduce.15.cloned.1.call-start
  92.0 1.7 convolution_convert_fusion
  93.7 0.0 all-reduce.15.cloned.1.call-update
  93.7 31.5 %all-reduce.13.cloned.1.call-done = f32[16,1024]{1,0:T(8,128)} async-done(((f32[16,1024]{1,0:T(8,128)}), f32[16,1024]{1,0:T(8,128)}) %all-reduce.13.cloned.1.call-update) | async-done | bytes 65552 | tf_op jit(solution)/shard_map/psum | solution.py:292
  125.2 0.8 multiply_convert_fusion.2
  126.1 0.1 convert_element_type.92
  126.2 1.0 copy.28
  127.2 1.9 pad_dynamic-slice_fusion.8
  129.1 1.1 copy.29
  130.2 1.1 copy.30
  131.3 1.1 copy.31
  132.4 1.1 copy.32
  133.4 1.1 copy.33
  134.5 1.1 copy.34
  135.6 1.1 copy.35
  136.8 1.1 copy.36
  137.9 0.1 copy.37
  138.1 1.5 fusion.61
  139.7 1.3 fusion.36.x_ref
  141.0 20.2 %reduce_small.1 = f32[32,8,128]{2,1,0:T(8,128)} custom-call(f32[32,8,128]{2,1,0:T(8,128)} %fusion.36.x_ref), custom_call_target="tpu_custom_call" | custom-call | tf_op jit(solution)/shard_map/reduce_small/pallas_call | solution.py:191
  161.2 0.9 slice.127
  162.1 0.7 slice.128
  162.8 1.2 slice.144
  164.6 1.4 convolution_convert_fusion.1
  166.0 100.0 %all-reduce.15.cloned.1.call-done = bf16[1024,768]{1,0:T(8,128)(2,1)} async-done(((bf16[1024,768]{1,0:T(8,128)(2,1)}), bf16[1024,768]{1,0:T(8,128)(2,1)}) %all-reduce.15.cloned.1.call-update) | async-done | bytes 1572880 | tf_op jit(solution)/shard_map/psum | solution.py:268
  266.0 3.3 %convert_element_type.97 = f32[1024,768]{1,0:T(8,128)} convert(bf16[1024,768]{1,0:T(8,128)(2,1)} %all-reduce.15.cloned.1.call-done) | non-fusion elementwise | flops 786432 | bytes 4718592 | tf_op jit(solution)/shard_map/convert_element_type | solution.py:268
  (44 shorter events, 0.3 us)
Async XLA Ops:
  7.2 48.8 %copy-start = (bf16[1024,1024]{1,0:T(8,128)(2,1)S(1)}, bf16[1024,1024]{1,0:T(8,128)(2,1)}, u32[]{:S(2)}) copy-start(bf16[1024,1024]{1,0:T(8,128)(2,1)} %param.15) | copy-start | bytes 6291460
  7.2 14.9 %copy-start.9 = (bf16[16,1024]{1,0:T(8,128)(2,1)S(1)}, bf16[16,1024]{1,0:T(8,128)(2,1)}, u32[]{:S(2)}) copy-start(bf16[16,1024]{1,0:T(8,128)(2,1)} %param.12) | copy-start | bytes 98308
  7.2 118.0 %all-reduce.13.cloned.1.call-start = ((), (), s32[]{:S(2)}) async-start(), calls=%async_computation | async-start | bytes 131072 | tf_op jit(solution)/shard_map/psum | solution.py:292
  22.9 2.0 copy-start.2
  55.9 2.5 copy-start.3
  55.9 2.5 copy-start.8
  58.4 2.3 copy-start.5
  78.2 4.8 %copy-start.1 = (f32[1024,1024]{0,1:T(8,128)S(1)}, f32[1024,1024]{0,1:T(8,128)}, u32[]{:S(2)}) copy-start(f32[1024,1024]{0,1:T(8,128)} %get-tuple-element.25) | copy-start | bytes 12582916
  78.2 4.8 %copy-start.4 = (bf16[1024,1024]{1,0:T(8,128)(2,1)S(1)}, bf16[1024,1024]{1,0:T(8,128)(2,1)}, u32[]{:S(2)}) copy-start(bf16[1024,1024]{1,0:T(8,128)(2,1)} %get-tuple-element.11) | copy-start | bytes 6291460
  82.9 4.4 %copy-start.10 = (bf16[16,1024]{1,0:T(8,128)(2,1)S(1)}, bf16[16,1024]{1,0:T(8,128)(2,1)}, u32[]{:S(2)}) copy-start(bf16[16,1024]{1,0:T(8,128)(2,1)} %param.12) | copy-start | bytes 98308
  87.4 1.0 copy-start.13
  88.1 2.7 copy-start.7
  88.4 3.6 %copy-start.6 = (bf16[256,1024]{0,1:T(8,128)(2,1)S(1)}, bf16[256,1024]{0,1:T(8,128)(2,1)}, u32[]{:S(2)}) copy-start(bf16[256,1024]{0,1:T(8,128)(2,1)} %copy-done.5) | copy-start | bytes 1572868
  90.8 2.9 %copy-start.12 = (bf16[9,512,4]{1,2,0:T(4,128)(2,1)S(1)}, bf16[9,512,4]{1,2,0:T(4,128)(2,1)}, u32[]{:S(2)}) copy-start(bf16[9,512,4]{1,2,0:T(4,128)(2,1)} %param.11) | copy-start | bytes 110596
  91.2 0.6 copy-start.11
  91.9 174.2 %all-reduce.15.cloned.1.call-start = ((), (), s32[]{:S(2)}) async-start(), calls=%async_computation.1 | async-start | bytes 3145728 | tf_op jit(solution)/shard_map/psum | solution.py:268
Sparse Core Ops, SparseCore 0:
  92.0 33.1 all-reduce.12
  131.1 134.9 all-reduce.14

commit v2 on v1

--- a/solution.py
+++ b/solution.py
@@ -122,83 +122,133 @@
     )(query, kv, kv, grad, attended, lse)
 
 
-def reduce_kernel(slabs, images, x_ref, out_ref, recv, send1, recv1, send2, recv2):
-    count = slabs * images
-    me = lax.axis_index("slab") * images + lax.axis_index("img")
-
-    def where(step):
-        peer = lax.rem(me + step, count)
-        return peer, {"slab": peer // images, "img": lax.rem(peer, images)}
-
-    barrier = pltpu.get_barrier_semaphore()
-
-    def hello(step, _):
-        _, spot = where(step)
-        pl.semaphore_signal(barrier, inc=1, device_id=spot, device_id_type=MESH_ID)
-        return 0
-
-    lax.fori_loop(1, count, hello, 0)
-    pl.semaphore_wait(barrier, count - 1)
-
-    def spread(step):
-        peer, spot = where(step)
-        return pltpu.make_async_remote_copy(
-            src_ref=x_ref.at[peer], dst_ref=recv.at[me], send_sem=send1.at[peer],
-            recv_sem=recv1.at[me], device_id=spot, device_id_type=MESH_ID)
-
-    def arrive(step):
-        peer, spot = where(step)
-        return pltpu.make_async_remote_copy(
-            src_ref=x_ref.at[peer], dst_ref=recv.at[peer], send_sem=send1.at[peer],
-            recv_sem=recv1.at[peer], device_id=spot, device_id_type=MESH_ID)
-
-    def share(step):
-        peer, spot = where(step)
-        return pltpu.make_async_remote_copy(
-            src_ref=out_ref.at[me], dst_ref=out_ref.at[me], send_sem=send2.at[peer],
-            recv_sem=recv2.at[me], device_id=spot, device_id_type=MESH_ID)
-
-    def landed(step):
-        peer, spot = where(step)
-        return pltpu.make_async_remote_copy(
-            src_ref=out_ref.at[me], dst_ref=out_ref.at[peer], send_sem=send2.at[peer],
-            recv_sem=recv2.at[peer], device_id=spot, device_id_type=MESH_ID)
+def reduce_kernel(chips, images, *refs):
+    size = (len(refs) - 8) // 5
+    xs, outs, near, half, recv = (refs[i * size : (i + 1) * size] for i in range(5))
+    send0, recv0, send1, recv1, send2, recv2, send3, recv3 = refs[5 * size :]
+    slab = lax.axis_index("slab")
+    image = lax.axis_index("img")
+    core = lax.rem(slab, 2)
+    me = (slab // 2) * images + image
+    partner = {"slab": slab + 1 - 2 * core, "img": image}
+
+    def spot(peer):
+        return {"slab": (peer // images) * 2 + core, "img": lax.rem(peer, images)}
 
     def each(body):
         def run(step, _):
-            body(step)
+            body(lax.rem(me + step, chips))
             return 0
 
-        lax.fori_loop(1, count, run, 0)
-
-    each(lambda step: spread(step).start())
-    each(lambda step: arrive(step).wait_recv())
-    total = x_ref[me]
-    total = lax.fori_loop(
-        1, count, lambda step, acc: acc + recv[lax.rem(me + step, count)], total)
-    out_ref[me] = total
-    each(lambda step: share(step).start())
-    each(lambda step: spread(step).wait_send())
-    each(lambda step: landed(step).wait_recv())
-    each(lambda step: share(step).wait_send())
-
-
-def reduce_small(flat, slabs, images):
-    count = slabs * images
-    rows = math.ceil(flat.size / count / 1024) * 8
-    cells = jnp.pad(flat, (0, count * rows * 128 - flat.size)).reshape(count, rows, 128)
+        lax.fori_loop(1, chips, run, 0)
+
+    def copy(src, dst, send, recv_sem, device):
+        return pltpu.make_async_remote_copy(
+            src_ref=src, dst_ref=dst, send_sem=send, recv_sem=recv_sem,
+            device_id=device, device_id_type=MESH_ID)
+
+    barrier = pltpu.get_barrier_semaphore()
+    pl.semaphore_signal(barrier, inc=1, device_id=partner, device_id_type=MESH_ID)
+    each(
+        lambda peer: pl.semaphore_signal(
+            barrier, inc=1, device_id=spot(peer), device_id_type=MESH_ID
+        )
+    )
+    pl.semaphore_wait(barrier, chips)
+
+    first = [
+        copy(xs[i].at[1 - core], near[i], send0.at[i], recv0.at[i], partner) for i in range(size)
+    ]
+    for c in first:
+        c.start()
+    for i in range(size):
+        first[i].wait_recv()
+        kind = half[i].dtype
+
+        def add(j, _, i=i, kind=kind):
+            both = xs[i][core, j].astype(jnp.float32) + near[i][j].astype(jnp.float32)
+            half[i][j] = both.astype(kind)
+            return 0
+
+        lax.fori_loop(0, chips, add, 0)
+        each(
+            lambda peer, i=i: copy(
+                half[i].at[peer], recv[i].at[me], send1.at[i, peer], recv1.at[i, me], spot(peer)
+            ).start()
+        )
+    for i in range(size):
+        each(
+            lambda peer, i=i: copy(
+                half[i].at[peer], recv[i].at[peer], send1.at[i, peer], recv1.at[i, peer],
+                spot(peer),
+            ).wait_recv()
+        )
+        total = lax.fori_loop(
+            1,
+            chips,
+            lambda step, acc, i=i: acc + recv[i][lax.rem(me + step, chips)].astype(jnp.float32),
+            half[i][me].astype(jnp.float32),
+        )
+        outs[i][core, me] = total.astype(outs[i].dtype)
+        each(
+            lambda peer, i=i: copy(
+                outs[i].at[core, me], outs[i].at[core, me], send2.at[i, peer], recv2.at[i, me],
+                spot(peer),
+            ).start()
+        )
+    last = [
+        copy(outs[i].at[core], outs[i].at[core], send3.at[i], recv3.at[i], partner)
+        for i in range(size)
+    ]
+    for i in range(size):
+        each(
+            lambda peer, i=i: copy(
+                outs[i].at[core, me], outs[i].at[core, peer], send2.at[i, peer],
+                recv2.at[i, peer], spot(peer),
+            ).wait_recv()
+        )
+        last[i].start()
+    for i in range(size):
+        first[i].wait_send()
+        each(
+            lambda peer, i=i: copy(
+                half[i].at[peer], recv[i].at[me], send1.at[i, peer], recv1.at[i, me], spot(peer)
+            ).wait_send()
+        )
+        each(
+            lambda peer, i=i: copy(
+                outs[i].at[core, me], outs[i].at[core, me], send2.at[i, peer], recv2.at[i, me],
+                spot(peer),
+            ).wait_send()
+        )
+        copy(
+            outs[i].at[core], outs[i].at[1 - core], send3.at[i], recv3.at[i], partner
+        ).wait_recv()
+        last[i].wait_send()
+
+
+def reduce_all(big, flat, slabs, images):
+    chips = slabs * images // 2
+    rows = math.ceil(flat.size / (2 * chips) / 1024) * 8
+    cells = jnp.pad(flat, (0, 2 * chips * rows * 128 - flat.size))
+    cells = cells.reshape(2, chips, rows, 128)
+    parts = [big.reshape(2, chips, -1, big.shape[1]), cells]
     vmem = pl.BlockSpec(memory_space=pltpu.VMEM)
+    shapes = [(p.shape, p.dtype) for p in parts]
+    dma = pltpu.SemaphoreType.DMA
     out = pl.pallas_call(
-        functools.partial(reduce_kernel, slabs, images),
-        out_shape=jax.ShapeDtypeStruct(cells.shape, cells.dtype),
-        in_specs=[vmem],
-        out_specs=vmem,
-        scratch_shapes=[pltpu.VMEM(cells.shape, cells.dtype)]
-        + [pltpu.SemaphoreType.DMA((count,))] * 4,
+        functools.partial(reduce_kernel, chips, images),
+        out_shape=[jax.ShapeDtypeStruct(*s) for s in shapes],
+        in_specs=[vmem] * 2,
+        out_specs=[vmem] * 2,
+        scratch_shapes=[pltpu.VMEM(s[1:], k) for s, k in shapes] * 3
+        + [dma((2,))] * 2
+        + [dma((2, chips))] * 4
+        + [dma((2,))] * 2,
         compiler_params=pltpu.CompilerParams(collective_id=0, has_side_effects=True),
-        name="reduce_small",
-    )(cells)
-    return out.reshape(-1)[: flat.size]
+        name="reduce_all",
+    )(*parts)
+    return out[0].reshape(big.shape), out[1].reshape(-1)[: flat.size]
 
 
 def cosine_grad(projected, target):
@@ -265,7 +315,6 @@
     cosine, grad_p = cosine_grad(projected, dino[0].astype(jnp.float32))
     grad_pb = grad_p.astype(jnp.bfloat16)
     proj_part = contract_first(resid_b, grad_pb).astype(jnp.bfloat16)
-    grad_proj = lax.psum(proj_part, ("slab", "img")).astype(jnp.float32)
     grad_resid = contract_last(grad_pb, proj_w)
     grad_att = contract_last(grad_resid.astype(jnp.bfloat16), out_w).astype(jnp.bfloat16)
     grad_query, grad_key, grad_value = attend_back(query, kv, grad_att, attended, lse)
@@ -289,7 +338,7 @@
     spread = spread + lax.dynamic_update_slice_in_dim(
         jnp.zeros_like(spread), spread_own, own, 1
     )
-    grad_tokens = lax.psum(spread, "slab")
+    grad_tokens = jnp.sum(lax.all_gather(spread, "slab", axis=0), 0)
     grad_latent = grad_tokens.reshape(2, 2, outs, full_rows // 2, cols // 2)
     grad_latent = grad_latent.transpose(2, 3, 0, 4, 1).reshape(outs, full_rows, cols)
     grad_latent = (grad_latent * latent_scale).astype(jnp.bfloat16)
@@ -307,9 +356,10 @@
     grad_image = contract_first(views, taps).astype(jnp.bfloat16).reshape(1, rows, cols, chans)
     conv_part = mm(views, cells, ((1,), (0,)))
     loss_part = jnp.sum(1.0 - cosine)
-    summed = reduce_small(
-        jnp.concatenate([conv_part.reshape(-1), loss_part[None]]), slabs, images
-    )
+    proj_sum, summed = reduce_all(
+        proj_part, jnp.concatenate([conv_part.reshape(-1), loss_part[None]]), slabs, images
+    )
+    grad_proj = proj_sum.astype(jnp.float32)
     grad_conv = summed[:-1].reshape(9, outs, chans).transpose(0, 2, 1)
     return (grad_image, grad_proj, grad_conv, summed[-1] / (slabs * images * count))
 

time: 278 us -> 179 us (0.64)
  waiting for transfers between devices: 132 us -> 0 us
  Pallas kernels: 49.1 us -> 81.5 us
  between operations: 17 us -> 3.55 us
  local copies, waits for them, and re-layouts: 23.9 us -> 30.2 us
  blocking collectives: 6.51 us -> 12.6 us
  matrix products: 36.6 us -> 39.5 us
    psum x2 -> x0, waiting for transfers between devices: 132 us -> none  [the longest x1 100 us: local(): grad_proj = lax.psum(proj_part, ('slab', 'img')).astype(jnp.float32)]
    pallas_call x1, Pallas kernels: 20.2 us -> 52.5 us  [reduce_all(): pl.pallas_call(functools.partial(reduce_kernel, chips, images), out_shape...]
    all_gather x0 -> x1, blocking collectives: none -> 6.12 us  [local(): grad_tokens = jnp.sum(lax.all_gather(spread, 'slab', axis=0), 0)]
    unnamed x39 -> x41, local copies, waits for them, and re-layouts: 3.01 us -> 7.15 us
  transfers between devices with their start and end apart: 2 -> 0, of which waited for: 2 -> 0; matrix products, arithmetic and copies ran while one was open for 8% -> 0% of each run, Pallas kernels for 7% -> 0%
where the time goes in v2:
time: 179 us; the launch traced here: 178 us
  Pallas kernels  81.5 us (46%)
  matrix products  39.5 us (22%)
  local copies, waits for them, and re-layouts  30.2 us (17%)
  blocking collectives  12.6 us (7%)
  other arithmetic  10.4 us (6%)
  between operations  3.55 us (2%)
    pallas_call x1, Pallas kernels, reduce_all(): pl.pallas_call(functools.partial(reduce_kernel, chips, images), out_shape...  52.5 us
    dot_general x11, matrix products, mm(): lax.dot_general(left, right, (dims, ((), ())), preferred_element_type=kind)  22.8 us
    pallas_call x1, Pallas kernels, attend_back(): pl.pallas_call(attend_back_kernel, grid=(pairs,), in_specs=[small, large,...  14.8 us
    pallas_call x1, Pallas kernels, attend(): pl.pallas_call(attend_kernel, grid=(pairs,), in_specs=[pl.BlockSpec((coun...  14.3 us
    slice x10, local copies, waits for them, and re-layouts, local(): grad_pad[:, 2 - ky:2 - ky + rows, 2 - kx:2 - kx + cols]  12 us
    dot_general x1, matrix products, local(): jnp.dot(modded, qkv_w[:, width:], preferred_element_type=jnp.float32)  9.37 us
    unnamed x41, local copies, waits for them, and re-layouts  7.15 us
    all_gather x1, blocking collectives, local(): terms_all = lax.all_gather(terms, 'slab', axis=0)  6.51 us

profile of v2, /device:TPU:0, one launch (start us, length us, event | category | flops | bytes accessed | tf_op | source)
XLA Modules:
  0.0 177.8 jit_solution(7199943873368754826)
XLA Ops:
  0.6 0.0 copy-start
  0.6 0.0 copy-start.10
  1.5 0.8 dynamic-slice_convert_fusion
  2.2 1.7 fusion.25
  3.9 0.1 fusion.50
  4.1 6.5 %all-gather = f32[16,10,128]{2,1,0:T(8,128)S(1)} all-gather(f32[4,10,128]{2,1,0:T(8,128)S(1)} %copy.27), channel_id=2, replica_groups=mesh['slab'=4,'img'=8] {'slab'}, dimensions={0}, use_global_device_ids=true | all-gather | bytes 102400 | tf_op jit(solution)/shard_map/all_gather | solution.py:278
  10.6 2.0 %copy.28 = f32[4,32,128]{0,2,1:T(8,128)} copy(f32[4,32,128]{2,1,0:T(8,128)S(1)} %fusion.48) | data formatting | bytes 131072 | tf_op jit(solution)/shard_map/mul | solution.py:280
  12.6 2.8 %copy.29 = f32[16,64,2,2,4]{1,0,4,3,2:T(8,128)S(1)} copy(f32[16,64,2,2,4]{4,3,1,2,0:T(2,128)} %bitcast.86) | data formatting | bytes 131072 | tf_op jit(solution)/shard_map/transpose | solution.py:284
  15.4 0.1 reshape.145
  15.5 0.8 fusion.58
  16.3 0.5 multiply_reduce_fusion.1
  16.8 3.4 %add_convert_fusion = (bf16[1024,1024]{0,1:T(8,128)(2,1)}, f32[1024,1024]{0,1:T(8,128)}) fusion(f32[1024]{0:T(1024)S(1)} %bitcast.103, f32[1024]{0:T(1024)S(1)} %bitcast.100, f32[1024]{0:T(1024)S(1)} %add_rsqrt_fusion, f32[1024,1024]{0,1:T(8,128)S(1)} %get-tuple-element.53, f32[1024]{0:T(1024)S(1)} %broadcast_multiply_fusion.2), kind=kLoop, calls=%fused_computation.5 | loop fusion | flops 5242880 | bytes 10502144 | tf_op jit(solution)/shard_map/convert_element_type | solution.py:302
  20.3 3.3 %fusion.19.q_ref = bf16[256,1024]{1,0:T(8,128)(2,1)} fusion(bf16[1024,3072]{1,0:T(8,128)(2,1)} %param.14, bf16[1024,1024]{0,1:T(8,128)(2,1)} %get-tuple-element.28, s32[]{:T(128)S(6)} %select_n.15), kind=kOutput, calls=%fused_computation.23 | convolution fusion | flops 537133056 | bytes 3145732 | tf_op jit(solution)/shard_map/dot_general | solution.py:308
  23.6 9.4 %fusion.2.k_ref.v_ref = bf16[1024,2048]{1,0:T(8,128)(2,1)} fusion(bf16[1024,1024]{0,1:T(8,128)(2,1)} %get-tuple-element.28, bf16[1024,3072]{1,0:T(8,128)(2,1)} %param.14), kind=kOutput, calls=%fused_computation.8 | convolution fusion | flops 4297064448 | bytes 10485760 | tf_op jit(solution)/shard_map/dot_general | solution.py:307
  32.9 14.3 %attend.1 = (bf16[256,1024]{1,0:T(8,128)(2,1)}, f32[8,2,256]{2,1,0:T(2,128)}) custom-call(bf16[256,1024]{1,0:T(8,128)(2,1)} %fusion.19.q_ref, bf16[1024,2048]{1,0:T(8,128)(2,1)} %fusion.2.k_ref.v_ref, bf16[1024,2048]{1,0:T(8,128)(2,1)} %fusion.2.k_ref.v_ref), custom_call_target="tpu_custom_call" | custom-call | flops 1073741824 | bytes 5242880 | tf_op jit(solution)/shard_map/attend/pallas_call | solution.py:73
  47.2 2.5 %fusion.22 = bf16[256,1024]{0,1:T(8,128)(2,1)S(1)} fusion(bf16[256,1024]{1,0:T(8,128)(2,1)} %get-tuple-element.11.o_ref, bf16[1024,1024]{1,0:T(8,128)(2,1)S(1)} %copy-done, f32[1024,1024]{0,1:T(8,128)} %copy-done.2, s32[]{:T(128)S(6)} %select_n.15), kind=kOutput, calls=%fused_computation.25 | convolution fusion | flops 537395200 | bytes 4194308 | tf_op jit(solution)/shard_map/dot_general | solution.py:312
  49.7 0.8 fusion.27
  50.5 0.6 subtract_reduce_fusion
  51.1 0.2 fusion.30
  51.4 0.6 fusion.59
  52.0 1.6 convolution_convert_fusion.2.g_ref
  53.5 14.8 %attend_back.1 = (bf16[256,1024]{1,0:T(8,128)(2,1)}, bf16[1024,1024]{1,0:T(8,128)(2,1)}, bf16[1024,1024]{1,0:T(8,128)(2,1)}) custom-call(bf16[256,1024]{1,0:T(8,128)(2,1)} %fusion.19.q_ref, bf16[1024,2048]{1,0:T(8,128)(2,1)} %fusion.2.k_ref.v_ref, bf16[1024,2048]{1,0:T(8,128)(2,1)} %fusion.2.k_ref.v_ref, bf16[256,1024]{1,0:T(8,128)(2,1)} %convolution_convert_fusion.2.g_ref, ...), custom_call_target="tpu_custom_call" | custom-call | flops 2684354560 | bytes 10485760 | tf_op jit(solution)/shard_map/attend_back/pallas_call | solution.py:103
  68.3 4.7 %fusion.5 = f32[1024,1024]{0,1:T(8,128)S(1)} fusion(bf16[1024,1024]{1,0:T(8,128)(2,1)} %get-tuple-element.14, bf16[1024,3072]{1,0:T(8,128)(2,1)} %param.14), kind=kOutput, calls=%fused_computation.9 | convolution fusion | flops 2147483648 | bytes 8388608 | tf_op jit(solution)/shard_map/dot_general | solution.py:22
  73.1 0.0 copy-start.11
  73.1 4.4 %fusion.55 = (f32[1024]{0:T(1024)S(1)}, f32[1024]{0:T(1024)S(1)}, f32[1024,1024]{0,1:T(8,128)S(1)}) fusion(f32[1024,1024]{0,1:T(8,128)S(1)} %copy-done.1, f32[1024]{0:T(1024)S(1)} %bitcast.101, f32[1024,1024]{0,1:T(8,128)S(1)} %fusion.5, bf16[1024,1024]{1,0:T(8,128)(2,1)S(1)} %copy-done.4, bf16[1024,3072]{1,0:T(8,128)(2,1)} %param.14), kind=kOutput, calls=%fused_computation.111 | convolution fusion | flops 2152724480 | bytes 16789504 | tf_op jit(solution)/shard_map/dot_general | solution.py:22
  77.5 0.8 fusion.9
  78.3 0.6 copy-done.9
  78.9 0.6 copy.48
  79.5 1.3 copy.32
  80.8 2.9 %fusion.56 = (f32[256]{0:T(256)S(1)}, f32[256]{0:T(256)S(1)}, f32[256,1024]{0,1:T(8,128)S(1)}) fusion(f32[1024,1024]{0,1:T(8,128)} %get-tuple-element.29, s32[]{:T(128)S(6)} %select_n.15, f32[1024]{0:T(1024)S(1)} %bitcast.102, bf16[256,1024]{1,0:T(8,128)(2,1)} %get-tuple-element.15, bf16[1024,3072]{1,0:T(8,128)(2,1)} %param.14), kind=kOutput, calls=%fused_computation.112 | convolution fusion | flops 537918976 | bytes 4724740 | tf_op jit(solution)/shard_map/dot_general | solution.py:22
  83.7 0.1 dynamic-slice.5
  83.8 1.6 fusion.24
  85.4 6.1 %all_gather.18 = f32[4,16,1024]{2,1,0:T(8,128)S(1)} all-gather(f32[1,16,1024]{2,1,0:T(8,128)S(1)} %fusion.24), channel_id=1, replica_groups=mesh['slab'=4,'img'=8] {'slab'}, dimensions={0}, use_global_device_ids=true | all-gather | bytes 327680 | tf_op jit(solution)/shard_map/all_gather | solution.py:341
  91.5 0.1 convert_element_type.95
  91.7 2.1 %copy.33 = bf16[4,16,2,64,2]{0,4,3,2,1:T(2,128)(2,1)} copy(bf16[4,16,2,64,2]{3,1,0,4,2:T(8,128)(2,1)S(1)} %bitcast.96) | data formatting | bytes 65536 | tf_op jit(solution)/shard_map/convert_element_type | solution.py:344
  93.8 4.2 %pad_dynamic-slice_fusion.8 = (bf16[4,8,128]{0,2,1:T(8,128)(2,1)S(1)}, bf16[4,8,128]{0,2,1:T(8,128)(2,1)}, bf16[4,8,128]{0,2,1:T(8,128)(2,1)}, bf16[4,8,128]{0,2...) fusion(s32[]{:T(128)S(6)} %select_n.16, ...), kind=kLoop, calls=%fused_computation.49 | loop fusion | bytes 106516 | tf_op jit(solution)/shard_map/slice | solution.py:350
  97.9 1.1 copy.34
  99.0 0.6 constant_dynamic-update-slice_fusion.8
  99.6 1.1 copy.35
  100.7 0.6 constant_dynamic-update-slice_fusion.7
  101.3 1.1 copy.36
  102.4 0.6 constant_dynamic-update-slice_fusion.6
  103.0 1.1 copy.37
  104.1 0.6 constant_dynamic-update-slice_fusion.5
  104.7 1.1 copy.38
  105.8 0.6 constant_dynamic-update-slice_fusion.4
  106.4 1.1 copy.39
  107.5 0.6 constant_dynamic-update-slice_fusion.3
  108.1 1.1 copy.40
  109.2 0.6 constant_dynamic-update-slice_fusion.2
  109.8 0.1 copy.41
  109.9 0.6 constant_dynamic-update-slice_fusion.1
  110.6 0.1 copy.42
  110.7 0.6 constant_dynamic-update-slice_fusion
  111.3 0.9 pad.64
  112.2 0.8 reshape.147
  113.0 1.4 convolution_convert_fusion.1
  114.5 1.7 convolution_convert_fusion
  116.2 1.5 fusion.60
  117.7 1.3 select_maximum_fusion
  119.0 52.5 %reduce_all.1 = (bf16[2,16,32,768]{3,2,1,0:T(8,128)(2,1)}, f32[2,16,8,128]{3,2,1,0:T(8,128)}) custom-call(bf16[2,16,32,768]{3,2,1,0:T(8,128)(2,1)} %bitcast.87, f32[2,16,8,128]{3,2,1,0:T(8,128)} %bitcast.93), custom_call_target="tpu_custom_call" | custom-call | tf_op jit(solution)/shard_map/reduce_all/pallas_call | solution.py:239
  171.5 3.3 %bitcast_convert_fusion = f32[1024,768]{1,0:T(8,128)} fusion(bf16[2,16,32,768]{3,2,1,0:T(8,128)(2,1)} %get-tuple-element.16), kind=kLoop, calls=%fused_computation.19 | loop fusion | flops 786432 | bytes 4718592 | tf_op jit(solution)/shard_map/convert_element_type | solution.py:362
  174.9 0.6 slice_bitcast_fusion
  175.5 0.5 slice.144
  (42 shorter events, 0.3 us)
Async XLA Ops:
  0.6 46.6 %copy-start = (bf16[1024,1024]{1,0:T(8,128)(2,1)S(1)}, bf16[1024,1024]{1,0:T(8,128)(2,1)}, u32[]{:S(2)}) copy-start(bf16[1024,1024]{1,0:T(8,128)(2,1)} %param.15) | copy-start | bytes 6291460
  0.6 14.9 %copy-start.10 = (bf16[16,1024]{1,0:T(8,128)(2,1)S(1)}, bf16[16,1024]{1,0:T(8,128)(2,1)}, u32[]{:S(2)}) copy-start(bf16[16,1024]{1,0:T(8,128)(2,1)} %param.12) | copy-start | bytes 98308
  16.3 4.0 %copy-start.2 = (f32[1024,1024]{0,1:T(8,128)}, f32[1024,1024]{0,1:T(8,128)S(1)}, u32[]{:S(2)}) copy-start(f32[1024,1024]{0,1:T(8,128)S(1)} %get-tuple-element.53) | copy-start | bytes 12582916
  47.2 2.5 %copy-start.3 = (bf16[1024,768]{1,0:T(8,128)(2,1)S(1)}, bf16[1024,768]{1,0:T(8,128)(2,1)}, u32[]{:S(2)}) copy-start(bf16[1024,768]{1,0:T(8,128)(2,1)} %param.16) | copy-start | bytes 4718596
  47.2 2.5 %copy-start.8 = (bf16[1,256,768]{2,1,0:T(8,128)(2,1)S(1)}, bf16[1,256,768]{2,1,0:T(8,128)(2,1)}, u32[]{:S(2)}) copy-start(bf16[1,256,768]{2,1,0:T(8,128)(2,1)} %param.17) | copy-start | bytes 1179652
  49.7 3.8 %copy-start.5 = (bf16[256,1024]{0,1:T(8,128)(2,1)}, bf16[256,1024]{0,1:T(8,128)(2,1)S(1)}, u32[]{:S(2)}) copy-start(bf16[256,1024]{0,1:T(8,128)(2,1)S(1)} %fusion.22) | copy-start | bytes 1572868
  68.3 4.8 %copy-start.1 = (f32[1024,1024]{0,1:T(8,128)S(1)}, f32[1024,1024]{0,1:T(8,128)}, u32[]{:S(2)}) copy-start(f32[1024,1024]{0,1:T(8,128)} %get-tuple-element.29) | copy-start | bytes 12582916
  68.3 4.8 %copy-start.4 = (bf16[1024,1024]{1,0:T(8,128)(2,1)S(1)}, bf16[1024,1024]{1,0:T(8,128)(2,1)}, u32[]{:S(2)}) copy-start(bf16[1024,1024]{1,0:T(8,128)(2,1)} %get-tuple-element.13) | copy-start | bytes 6291460
  73.1 4.4 %copy-start.11 = (bf16[16,1024]{1,0:T(8,128)(2,1)S(1)}, bf16[16,1024]{1,0:T(8,128)(2,1)}, u32[]{:S(2)}) copy-start(bf16[16,1024]{1,0:T(8,128)(2,1)} %param.12) | copy-start | bytes 98308
  78.2 0.6 copy-start.9
  80.8 3.0 %copy-start.7 = (f32[256,1024]{0,1:T(8,128)S(1)}, f32[256,1024]{0,1:T(8,128)}, u32[]{:S(2)}) copy-start(f32[256,1024]{0,1:T(8,128)} %copy.32) | copy-start | bytes 3145732
  80.8 3.0 %copy-start.12 = (bf16[16,1024]{1,0:T(8,128)(2,1)S(1)}, bf16[16,1024]{1,0:T(8,128)(2,1)}, u32[]{:S(2)}) copy-start(bf16[16,1024]{1,0:T(8,128)(2,1)} %param.12) | copy-start | bytes 98308
  80.8 3.0 %copy-start.13 = (f32[1,16,1024]{2,1,0:T(8,128)S(1)}, f32[1,16,1024]{2,1,0:T(8,128)}, u32[]{:S(2)}) copy-start(f32[1,16,1024]{2,1,0:T(8,128)} %copy.48) | copy-start | bytes 196612
  91.6 22.8 %copy-start.6 = (bf16[256,1024]{0,1:T(8,128)(2,1)S(1)}, bf16[256,1024]{0,1:T(8,128)(2,1)}, u32[]{:S(2)}) copy-start(bf16[256,1024]{0,1:T(8,128)(2,1)} %copy-done.5) | copy-start | bytes 1572868
  171.5 3.4 %copy-start.14 = (f32[2,16,8,128]{3,2,1,0:T(8,128)S(1)}, f32[2,16,8,128]{3,2,1,0:T(8,128)}, u32[]{:S(2)}) copy-start(f32[2,16,8,128]{3,2,1,0:T(8,128)} %get-tuple-element.17) | copy-start | bytes 393220
